TPU v7x, 64 devices: a 2x2x8 block of a 4x4x8 slice. The times are simulated.
64 devices in a mesh: dp: 8 (over x, y, core), tp: 8 (over z).
Axes of the slice: x: 2, y: 2, z: 8, core: 2. Of those that a mesh axis runs over, the one named last changes fastest.
The devices are a block of a 4x4x8 slice.
Arguments:
- x: bfloat16 [16384, 4096], P(('dp', 'tp')), parts along dimension 0
- w_gate: bfloat16 [4096, 16384], P(None, 'tp')
- w_up: bfloat16 [4096, 16384], P(None, 'tp')
- w_down: bfloat16 [16384, 4096], P('tp')
Outputs:
- output: bfloat16 [16384, 4096], P(('dp', 'tp')), parts along dimension 0
There are 8 independent parts. A program takes and returns all parts, laid end to end along the dimension named above; an argument that names none is the same for every part.
All inputs are finite; a program needn't handle non-finite values.
Results may differ from a plain program's by a relative error of at most 0.016.
Values are sent between devices in bfloat16 or wider.
A program may use at most 768 MiB of HBM per device.

v0:
```python
import jax
import jax.numpy as jnp
from jax import lax
from jax.sharding import PartitionSpec as P


def solution(mesh):
    def step(x, w_gate, w_up, w_down):
        rows = lax.all_gather(x, "tp", axis=0, tiled=True)
        gate = jnp.dot(rows, w_gate, preferred_element_type=jnp.float32)
        up = jnp.dot(rows, w_up, preferred_element_type=jnp.float32)
        hidden = (jax.nn.silu(gate) * up).astype(jnp.bfloat16)
        term = jnp.dot(hidden, w_down, preferred_element_type=jnp.float32).astype(jnp.bfloat16)
        return lax.psum_scatter(term, "tp", scatter_dimension=0, tiled=True)

    return jax.shard_map(
        step,
        mesh=mesh,
        in_specs=(P(("dp", "tp"), None), P(None, "tp"), P(None, "tp"), P("tp", None)),
        out_specs=P(("dp", "tp"), None),
        check_vma=False,
    )
```

profile of v0, /device:TPU:21, one launch (start us, length us, event | category | flops | bytes accessed | tf_op | source)
XLA Modules:
  0.0 489.3 jit_solution(16671378231941476316)
XLA Ops:
  6.5 0.0 all-gather.2.cloned.1.call-start
  6.6 0.7 all-gather.2.cloned.1.call-update
  7.3 0.1 reduce-scatter.2.cloned.1.call-start
  7.4 175.3 %all-gather.2.cloned.1.call-done = bf16[2048,4096]{1,0:T(8,128)(2,1)} async-done(((bf16[256,4096]{1,0:T(8,128)(2,1)}), bf16[2048,4096]{1,0:T(8,128)(2,1)}) %all-gather.2.cloned.1.call-update) | async-done | bytes 16777232 | tf_op jit(solution)/shard_map/all_gather | solution.py:9
  182.7 43.0 %fusion = f32[2048,2048]{1,0:T(8,128)} fusion(bf16[2048,4096]{1,0:T(8,128)(2,1)} %all-gather.2.cloned.1.call-done, bf16[4096,2048]{1,0:T(8,128)(2,1)} %param.5), kind=kOutput, calls=%fused_computation.2 | convolution fusion | flops 34359738368 | bytes 50331648 | tf_op jit(solution)/shard_map/dot_general | solution.py:10
  225.7 46.7 %multiply_convert_fusion = bf16[2048,2048]{1,0:T(8,128)(2,1)S(1)} fusion(f32[2048,2048]{1,0:T(8,128)} %fusion, bf16[2048,4096]{1,0:T(8,128)(2,1)} %all-gather.2.cloned.1.call-done, bf16[4096,2048]{1,0:T(8,128)(2,1)} %param.6), kind=kOutput, calls=%fused_computation | convolution fusion | flops 34384904192 | bytes 58720256 | tf_op jit(solution)/shard_map/dot_general | solution.py:11
  272.4 41.0 %convolution_convert_fusion = bf16[2048,4096]{1,0:T(8,128)(2,1)} fusion(bf16[2048,2048]{1,0:T(8,128)(2,1)S(1)} %multiply_convert_fusion, bf16[2048,4096]{1,0:T(8,128)(2,1)} %param.7), kind=kOutput, calls=%fused_computation.1 | convolution fusion | flops 34368126976 | bytes 41943040 | tf_op jit(solution)/shard_map/dot_general | solution.py:13
  313.4 0.1 reduce-scatter.2.cloned.1.call-update
  313.5 169.0 %reduce-scatter.2.cloned.1.call-done = bf16[256,4096]{1,0:T(8,128)(2,1)} async-done(((bf16[2048,4096]{1,0:T(8,128)(2,1)}), bf16[256,4096]{1,0:T(8,128)(2,1)}) %reduce-scatter.2.cloned.1.call-update) | async-done | bytes 2097168 | tf_op jit(solution)/shard_map/reduce_scatter | solution.py:14
Async XLA Ops:
  6.5 176.1 %all-gather.2.cloned.1.call-start = ((), (), s32[]{:S(2)}) async-start(), calls=%async_computation.1 | async-start | bytes 18874368 | tf_op jit(solution)/shard_map/all_gather | solution.py:9
  7.3 475.2 %reduce-scatter.2.cloned.1.call-start = ((), (), s32[]{:S(2)}) async-start(), calls=%async_computation.2 | async-start | bytes 18874368 | tf_op jit(solution)/shard_map/reduce_scatter | solution.py:14
Sparse Core Ops, SparseCore 0:
  8.9 173.7 all-gather.1
  313.6 168.8 reduce-scatter.1
where the time goes:
time: 489 us
  waiting for transfers between devices  345 us (71%)
  matrix products  131 us (27%)
  between operations  13.4 us (3%)
    all_gather x1, waiting for transfers between devices, step(): rows = lax.all_gather(x, 'tp', axis=0, tiled=True)  175 us
    reduce_scatter x1, waiting for transfers between devices, step(): return lax.psum_scatter(term, 'tp', scatter_dimension=0, tiled=True)  169 us
    dot_general x1, matrix products, step(): up = jnp.dot(rows, w_up, preferred_element_type=jnp.float32)  46.7 us
    dot_general x1, matrix products, step(): gate = jnp.dot(rows, w_gate, preferred_element_type=jnp.float32)  43 us
    dot_general x1, matrix products, step(): jnp.dot(hidden, w_down, preferred_element_type=jnp.float32)  41 us
  transfers between devices with their start and end apart: 2, of which 2 were waited for; matrix products, arithmetic and copies ran while one was open for 0% of the time, Pallas kernels for 0%

commit v1 on v0

v1 whole, which is shorter than its diff:
```python
import jax
import jax.numpy as jnp
from jax import lax
from jax.sharding import PartitionSpec as P

CHUNKS = 2


def solution(mesh):
    def mlp(rows, w_gate, w_up, w_down):
        gate = jnp.dot(rows, w_gate, preferred_element_type=jnp.float32)
        up = jnp.dot(rows, w_up, preferred_element_type=jnp.float32)
        hidden = (jax.nn.silu(gate) * up).astype(jnp.bfloat16)
        return jnp.dot(hidden, w_down, preferred_element_type=jnp.float32).astype(jnp.bfloat16)

    def step(x, w_gate, w_up, w_down):
        size = x.shape[0] // CHUNKS
        rows = [
            lax.all_gather(x[c * size : (c + 1) * size], "tp", axis=0, tiled=True)
            for c in range(CHUNKS)
        ]
        done = []
        for c in range(CHUNKS):
            term = mlp(rows[c], w_gate, w_up, w_down)
            done.append(lax.psum_scatter(term, "tp", scatter_dimension=0, tiled=True))
        return jnp.concatenate(done, axis=0)

    return jax.shard_map(
        step,
        mesh=mesh,
        in_specs=(P(("dp", "tp"), None), P(None, "tp"), P(None, "tp"), P("tp", None)),
        out_specs=P(("dp", "tp"), None),
        check_vma=False,
    )
```

time: 489 us -> 391 us (0.80)
  waiting for transfers between devices: 345 us -> 234 us
  matrix products: 131 us -> 137 us
    all_gather x1 -> x2, waiting for transfers between devices: 175 us -> 116 us  [step(): lax.all_gather(x[c * size:(c + 1) * size], 'tp', axis=0, tiled=True)]
    reduce_scatter x1 -> x2, waiting for transfers between devices: 169 us -> 116 us  [step(): done.append(lax.psum_scatter(term, 'tp', scatter_dimension=0, tiled=True))]
    dot_general x3 -> x6, matrix products: 131 us -> 137 us  [the longest x2 48.4 us: mlp(): gate = jnp.dot(rows, w_gate, preferred_element_type=jnp.float32)]
  transfers between devices with their start and end apart: 2 -> 4, of which waited for: 2 -> 4; matrix products, arithmetic and copies ran while one was open for 0% -> 35% of each run, Pallas kernels for 0% -> 0%
where the time goes in v1:
time: 391 us
  waiting for transfers between devices  234 us (60%)
  matrix products  137 us (35%)
  between operations  13.2 us (3%)
    reduce_scatter x2, waiting for transfers between devices, step(): done.append(lax.psum_scatter(term, 'tp', scatter_dimension=0, tiled=True))  116 us
    all_gather x2, waiting for transfers between devices, step(): lax.all_gather(x[c * size:(c + 1) * size], 'tp', axis=0, tiled=True)  116 us
    dot_general x2, matrix products, mlp(): gate = jnp.dot(rows, w_gate, preferred_element_type=jnp.float32)  48.4 us
    dot_general x2, matrix products, mlp(): up = jnp.dot(rows, w_up, preferred_element_type=jnp.float32)  46.1 us
    dot_general x2, matrix products, mlp(): jnp.dot(hidden, w_down, preferred_element_type=jnp.float32)  42.7 us
  transfers between devices with their start and end apart: 4, of which 4 were waited for; matrix products, arithmetic and copies ran while one was open for 35% of the time, Pallas kernels for 0%

profile of v1, /device:TPU:21, one launch (start us, length us, event | category | flops | bytes accessed | tf_op | source)
XLA Modules:
  0.0 390.6 jit_solution(1431382566694197422)
XLA Ops:
  6.5 0.0 all-gather.3.cloned.1.call-start
  6.6 3.1 fusion
  9.6 0.1 all-gather.3.cloned.1.call-update
  9.7 0.1 all-gather.5.cloned.1.call-start
  9.8 0.7 all-gather.5.cloned.1.call-update
  10.5 0.1 reduce-scatter.3.cloned.1.call-start
  10.6 94.4 %all-gather.3.cloned.1.call-done = bf16[1024,4096]{1,0:T(8,128)(2,1)} async-done(((bf16[128,4096]{1,0:T(8,128)(2,1)}), bf16[1024,4096]{1,0:T(8,128)(2,1)}) %all-gather.3.cloned.1.call-update) | async-done | bytes 8388624 | tf_op jit(solution)/shard_map/all_gather | solution.py:19
  104.9 0.0 copy-start.1
  104.9 0.0 slice-start
  105.0 0.0 slice-start.1
  105.0 24.2 %fusion.1 = f32[1024,2048]{1,0:T(8,128)} fusion(bf16[1024,4096]{1,0:T(8,128)(2,1)} %all-gather.3.cloned.1.call-done, bf16[4096,2048]{1,0:T(8,128)(2,1)} %param.5), kind=kOutput, calls=%fused_computation.6 | convolution fusion | flops 17179869184 | bytes 33554432 | tf_op jit(solution)/shard_map/dot_general | solution.py:11
  129.1 0.0 copy-done.1
  129.1 0.0 slice-start.2
  129.1 0.0 slice-start.3
  129.1 23.1 %multiply_convert_fusion.1 = bf16[1024,2048]{1,0:T(8,128)(2,1)} fusion(f32[1024,2048]{1,0:T(8,128)} %fusion.1, bf16[1024,4096]{1,0:T(8,128)(2,1)S(1)} %copy-done.1, bf16[4096,2048]{1,0:T(8,128)(2,1)} %param.6), kind=kOutput, calls=%fused_computation.1 | convolution fusion | flops 17192452096 | bytes 37748736 | tf_op jit(solution)/shard_map/dot_general | solution.py:12
  152.2 0.0 slice-done
  152.2 0.0 slice-done.1
  152.2 0.0 slice-done.2
  152.2 0.0 slice-done.3
  152.2 21.4 %convolution_convert_fusion.1 = bf16[1024,4096]{1,0:T(8,128)(2,1)} fusion(bf16[1024,2048]{1,0:T(8,128)(2,1)} %multiply_convert_fusion.1, bf16[2048,4096]{1,0:T(8,128)(2,1)S(1)} %bitcast.13), kind=kOutput, calls=%fused_computation.3 | convolution fusion | flops 17184063488 | bytes 29360128 | tf_op jit(solution)/shard_map/dot_general | solution.py:14
  173.6 0.1 reduce-scatter.3.cloned.1.call-update
  173.7 0.2 reduce-scatter.5.cloned.1.call-start
  173.9 21.9 %all-gather.5.cloned.1.call-done = bf16[1024,4096]{1,0:T(8,128)(2,1)} async-done(((bf16[128,4096]{1,0:T(8,128)(2,1)}), bf16[1024,4096]{1,0:T(8,128)(2,1)}) %all-gather.5.cloned.1.call-update) | async-done | bytes 8388624 | tf_op jit(solution)/shard_map/all_gather | solution.py:19
  195.8 0.0 copy-start
  195.8 0.0 slice-start.4
  195.8 0.0 slice-start.5
  195.8 24.2 %fusion.2 = f32[1024,2048]{1,0:T(8,128)} fusion(bf16[1024,4096]{1,0:T(8,128)(2,1)} %all-gather.5.cloned.1.call-done, bf16[4096,2048]{1,0:T(8,128)(2,1)} %param.5), kind=kOutput, calls=%fused_computation.7 | convolution fusion | flops 17179869184 | bytes 33554432 | tf_op jit(solution)/shard_map/dot_general | solution.py:11
  220.0 0.0 copy-done
  220.0 0.0 slice-start.6
  220.0 0.0 slice-start.7
  220.0 23.1 %multiply_convert_fusion = bf16[1024,2048]{1,0:T(8,128)(2,1)} fusion(f32[1024,2048]{1,0:T(8,128)} %fusion.2, bf16[1024,4096]{1,0:T(8,128)(2,1)S(1)} %copy-done, bf16[4096,2048]{1,0:T(8,128)(2,1)} %param.6), kind=kOutput, calls=%fused_computation | convolution fusion | flops 17192452096 | bytes 37748736 | tf_op jit(solution)/shard_map/dot_general | solution.py:12
  243.1 0.0 slice-done.4
  243.1 0.0 slice-done.5
  243.1 0.0 slice-done.6
  243.1 0.0 slice-done.7
  243.1 21.3 %convolution_convert_fusion = bf16[1024,4096]{1,0:T(8,128)(2,1)} fusion(bf16[1024,2048]{1,0:T(8,128)(2,1)} %multiply_convert_fusion, bf16[2048,4096]{1,0:T(8,128)(2,1)S(1)} %bitcast.15), kind=kOutput, calls=%fused_computation.2 | convolution fusion | flops 17184063488 | bytes 29360128 | tf_op jit(solution)/shard_map/dot_general | solution.py:14
  264.5 0.1 reduce-scatter.5.cloned.1.call-update
  264.5 23.9 %reduce-scatter.3.cloned.1.call-done = bf16[128,4096]{1,0:T(8,128)(2,1)} async-done(((bf16[1024,4096]{1,0:T(8,128)(2,1)}), bf16[128,4096]{1,0:T(8,128)(2,1)}) %reduce-scatter.3.cloned.1.call-update) | async-done | bytes 1048592 | tf_op jit(solution)/shard_map/reduce_scatter | solution.py:25
  288.4 92.5 %reduce-scatter.5.cloned.1.call-done = bf16[128,4096]{1,0:T(8,128)(2,1)} async-done(((bf16[1024,4096]{1,0:T(8,128)(2,1)}), bf16[128,4096]{1,0:T(8,128)(2,1)}) %reduce-scatter.5.cloned.1.call-update) | async-done | bytes 1048592 | tf_op jit(solution)/shard_map/reduce_scatter | solution.py:25
  380.9 3.1 pad_maximum_fusion
  (2 shorter events, 0.0 us)
Async XLA Ops:
  6.5 98.4 %all-gather.3.cloned.1.call-start = ((), (), s32[]{:S(2)}) async-start(), calls=%async_computation.2 | async-start | bytes 9437184 | tf_op jit(solution)/shard_map/all_gather | solution.py:19
  9.7 186.1 %all-gather.5.cloned.1.call-start = ((), (), s32[]{:S(2)}) async-start(), calls=%async_computation.4 | async-start | bytes 9437184 | tf_op jit(solution)/shard_map/all_gather | solution.py:19
  10.5 277.9 %reduce-scatter.3.cloned.1.call-start = ((), (), s32[]{:S(2)}) async-start(), calls=%async_computation.3 | async-start | bytes 9437184 | tf_op jit(solution)/shard_map/reduce_scatter | solution.py:25
  104.9 24.2 %copy-start.1 = (bf16[1024,4096]{1,0:T(8,128)(2,1)S(1)}, bf16[1024,4096]{1,0:T(8,128)(2,1)}, u32[]{:S(2)}) copy-start(bf16[1024,4096]{1,0:T(8,128)(2,1)} %all-gather.3.cloned.1.call-done) | copy-start | bytes 25165828
  104.9 47.3 %slice-start = ((s8[16777216]{0:T(1024)(128)(4,1)}), s8[4194304]{0:T(1024)(128)(4,1)S(1)}, s32[]{:S(2)}) async-start(s8[16777216]{0:T(1024)(128)(4,1)} %bitcast.12), calls=%async_computation.6 | async-start | bytes 8388608
  105.0 47.3 %slice-start.1 = ((s8[16777216]{0:T(1024)(128)(4,1)}), s8[4194304]{0:T(1024)(128)(4,1)S(1)}, s32[]{:S(2)}) async-start(s8[16777216]{0:T(1024)(128)(4,1)} %bitcast.12), calls=%async_computation.7 | async-start | bytes 8388608
  129.1 23.1 %slice-start.2 = ((s8[16777216]{0:T(1024)(128)(4,1)}), s8[4194304]{0:T(1024)(128)(4,1)S(1)}, s32[]{:S(2)}) async-start(s8[16777216]{0:T(1024)(128)(4,1)} %bitcast.12), calls=%async_computation.8 | async-start | bytes 8388608
  129.1 23.1 %slice-start.3 = ((s8[16777216]{0:T(1024)(128)(4,1)}), s8[4194304]{0:T(1024)(128)(4,1)S(1)}, s32[]{:S(2)}) async-start(s8[16777216]{0:T(1024)(128)(4,1)} %bitcast.12), calls=%async_computation.9 | async-start | bytes 8388608
  173.7 207.2 %reduce-scatter.5.cloned.1.call-start = ((), (), s32[]{:S(2)}) async-start(), calls=%async_computation.5 | async-start | bytes 9437184 | tf_op jit(solution)/shard_map/reduce_scatter | solution.py:25
  195.8 24.2 %copy-start = (bf16[1024,4096]{1,0:T(8,128)(2,1)S(1)}, bf16[1024,4096]{1,0:T(8,128)(2,1)}, u32[]{:S(2)}) copy-start(bf16[1024,4096]{1,0:T(8,128)(2,1)} %all-gather.5.cloned.1.call-done) | copy-start | bytes 25165828
  195.8 47.3 %slice-start.4 = ((s8[16777216]{0:T(1024)(128)(4,1)}), s8[4194304]{0:T(1024)(128)(4,1)S(1)}, s32[]{:S(2)}) async-start(s8[16777216]{0:T(1024)(128)(4,1)} %bitcast.14), calls=%async_computation.10 | async-start | bytes 8388608
  195.8 47.3 %slice-start.5 = ((s8[16777216]{0:T(1024)(128)(4,1)}), s8[4194304]{0:T(1024)(128)(4,1)S(1)}, s32[]{:S(2)}) async-start(s8[16777216]{0:T(1024)(128)(4,1)} %bitcast.14), calls=%async_computation.11 | async-start | bytes 8388608
  220.0 23.1 %slice-start.6 = ((s8[16777216]{0:T(1024)(128)(4,1)}), s8[4194304]{0:T(1024)(128)(4,1)S(1)}, s32[]{:S(2)}) async-start(s8[16777216]{0:T(1024)(128)(4,1)} %bitcast.14), calls=%async_computation.12 | async-start | bytes 8388608
  220.0 23.1 %slice-start.7 = ((s8[16777216]{0:T(1024)(128)(4,1)}), s8[4194304]{0:T(1024)(128)(4,1)S(1)}, s32[]{:S(2)}) async-start(s8[16777216]{0:T(1024)(128)(4,1)} %bitcast.14), calls=%async_computation.13 | async-start | bytes 8388608
Sparse Core Ops, SparseCore 0:
  9.8 95.0 all-gather.2
  106.5 89.2 all-gather.4
  198.2 90.2 reduce-scatter.2
  290.6 90.2 reduce-scatter.4

commit v2 on v0

v2 whole, which is shorter than its diff:
```python
import functools

import jax
import jax.numpy as jnp
from jax import lax
from jax.experimental import pallas as pl
from jax.experimental.pallas import tpu as pltpu
from jax.sharding import PartitionSpec as P

MESH = pl.DeviceIdType.MESH
F32 = jnp.float32
BF16 = jnp.bfloat16
FT = 256
SLOTS = 3
NT = 512


def kernel(
    n, x_ref, wg_ref, wu_ref, wd_ref, y_ref,
    buf, hid, wd, wt, own, ag_send, ag_recv, rs_send, rs_recv, w_sem, wd_sem, x_sem, y_sem,
):
    me = lax.axis_index("tp")
    right, left = lax.rem(me + 1, n), lax.rem(me + n - 1, n)
    steps = n - 1
    rc = x_ref.shape[0] // 2
    pc = rc // 2
    d_model = x_ref.shape[1]
    ff = wg_ref.shape[1]
    tiles = ff // FT
    per = tiles // 2
    n_tiles = 2 * n * per

    def rows(block, part=0, size=pc):
        return pl.ds(pl.multiple_of(block * rc + part * pc, pc), size)

    def own_block(c):
        return 2 * n - 1 - n * c

    def ag_copy(d, c, i, src):
        return pltpu.make_async_remote_copy(
            src_ref=buf.at[src],
            dst_ref=buf.at[rows(c * n + i, d)],
            send_sem=ag_send.at[d, c * steps + i],
            recv_sem=ag_recv.at[d, c * steps + i],
            device_id={"tp": (right, left)[d]},
            device_id_type=MESH,
        )

    def arrived_sum(c, r):
        return 2 * n * (1 - c) + r

    def rs_copy(d, c, r, block):
        return pltpu.make_async_remote_copy(
            src_ref=buf.at[rows(block, d)],
            dst_ref=buf.at[rows(arrived_sum(c, r), d)],
            send_sem=rs_send.at[d, c * steps + r],
            recv_sem=rs_recv.at[d, c * steps + r],
            device_id={"tp": (left, right)[d]},
            device_id_type=MESH,
        )

    def w_copies(g):
        slot = g % SLOTS
        col = pl.ds(pl.multiple_of((g % tiles) * FT, FT), FT)
        return [
            pltpu.make_async_copy(ref.at[:, col], wt.at[slot, :, pl.ds(k * FT, FT)], w_sem.at[k, slot])
            for k, ref in enumerate((wg_ref, wu_ref))
        ]

    x_copies = [
        pltpu.make_async_copy(
            x_ref.at[pl.ds(c * rc, rc)], buf.at[rows(own_block(c), 0, rc)], x_sem.at[c]
        )
        for c in range(2)
    ]
    for copy in x_copies:
        copy.start()

    barrier = pltpu.get_barrier_semaphore()
    for neighbour in (left, right):
        pl.semaphore_signal(barrier, inc=1, device_id={"tp": neighbour}, device_id_type=MESH)
    pl.semaphore_wait(barrier, 2)

    def send_own(c):
        for i in range(2):
            for d in range(2):
                ag_copy(d, c, i, rows(own_block(c), i ^ d)).start()

    x_copies[0].wait()
    send_own(0)
    x_copies[1].wait()
    for g in range(SLOTS - 1):
        for copy in w_copies(g):
            copy.start()
    wd_copy = pltpu.make_async_copy(wd_ref, wd, wd_sem)
    wd_copy.start()

    def hidden_half(q):
        lhs = pl.ds(pl.multiple_of((q // 2) * 2 * rc, 2 * rc), 2 * rc)

        @pl.loop(0, per)
        def _(j):
            g = q * per + j
            slot = g % SLOTS
            for copy in w_copies(g):
                copy.wait()

            @pl.when(g + SLOTS - 1 < n_tiles)
            def _():
                for copy in w_copies(g + SLOTS - 1):
                    copy.start()

            both = jnp.dot(buf[lhs, :], wt[slot], preferred_element_type=F32)
            gate, up = both[:, :FT], both[:, FT:]
            col = pl.ds(pl.multiple_of((g % tiles) * FT, FT), FT)
            hid[lhs, col] = (jax.nn.silu(gate) * up).astype(BF16)

    def down(block, col):
        return jnp.dot(hid[rows(block, 0, rc), :], wd[:, col], preferred_element_type=F32)

    def down_tiles(body):
        @pl.loop(0, d_model // NT)
        def _(j):
            body(pl.ds(pl.multiple_of(j * NT, NT), NT))

    def send_sum(c, r, add):
        block = arrived_sum(c, r - 2) if add else c * n + n - 2 + r
        dst = rows(block, 0, rc)

        def body(col):
            term = down(c * n + n - 2 - r, col)
            if add:
                term = term + buf[dst, col].astype(F32)
            buf[dst, col] = term.astype(BF16)

        down_tiles(body)
        for d in range(2):
            rs_copy(d, c, r, block).start()

    def wait_sum(c, r):
        for d in range(2):
            rs_copy(d, c, r, arrived_sum(c, r)).wait_recv()

    def swapped(block, col):
        return jnp.concatenate([buf[rows(block, 1), col], buf[rows(block, 0), col]], axis=0).astype(F32)

    def y_copy(c):
        return pltpu.make_async_copy(
            buf.at[rows(arrived_sum(c, steps - 1), 0, rc)], y_ref.at[pl.ds(c * rc, rc)], y_sem.at[c]
        )

    @pl.loop(0, 4 * steps - 2)
    def _(t):
        @pl.when(t < 2 * steps)
        def _():
            c, i = t // steps, t % steps
            for d in range(2):
                ag_copy(d, c, i, rows(c * n + i, d)).wait_recv()

            @pl.when(i < steps - 2)
            def _():
                for d in range(2):
                    ag_copy(d, c, i + 2, rows(c * n + i, d)).start()

        @pl.when(t == steps - 2)
        def _():
            send_own(1)

        @pl.when((t >= 1) & (t <= 2 * steps))
        def _():
            a = t - 1
            for d in range(2):
                ag_copy(d, a // steps, a % steps, rows((a // steps) * n + a % steps, d)).wait_send()

        @pl.when(t >= 2 * steps + 1)
        def _():
            u = t - (2 * steps + 1)
            for d in range(2):
                rs_copy(d, u // steps, u % steps, arrived_sum(u // steps, u % steps)).wait_send()

        @pl.when(t == 2 * steps - 2)
        def _():
            wd_copy.wait()

        @pl.when(t >= 2 * steps - 2)
        def _():
            u = t - (2 * steps - 2)
            c, r = u // steps, u % steps

            @pl.when(r < 2)
            def _():
                send_sum(c, r, False)

            @pl.when(r >= 2)
            def _():
                wait_sum(c, r - 2)
                send_sum(c, r, True)

        @pl.when((t >= 1) & (t <= 2 * n))
        def _():
            hidden_half(t - 1)

        @pl.when(t == 3 * steps - 1)
        def _():
            wait_sum(0, steps - 2)
            wait_sum(0, steps - 1)
            last = arrived_sum(0, steps - 1)
            dst = rows(last, 0, rc)

            def body(col):
                total = down(own_block(0), col) + swapped(last - 1, col) + buf[dst, col].astype(F32)
                buf[dst, col] = total.astype(BF16)

            down_tiles(body)
            y_copy(0).start()

    wait_sum(1, steps - 2)
    last = arrived_sum(1, steps - 1)
    dst = rows(last, 0, rc)

    def partial(col):
        own[:, col] = down(own_block(1), col) + swapped(last - 1, col)

    down_tiles(partial)
    wait_sum(1, steps - 1)

    def finish(col):
        buf[dst, col] = (own[:, col] + buf[dst, col].astype(F32)).astype(BF16)

    down_tiles(finish)
    y_copy(1).start()
    for u in range(2 * steps - 3, 2 * steps):
        for d in range(2):
            rs_copy(d, u // steps, u % steps, arrived_sum(u // steps, u % steps)).wait_send()
    for c in range(2):
        y_copy(c).wait()


def solution(mesh):
    n = mesh.shape["tp"]

    def step(x, w_gate, w_up, w_down):
        (m, d_model), ff = x.shape, w_gate.shape[1]
        rc = m // 2
        steps = n - 1
        hbm = pl.BlockSpec(memory_space=pltpu.HBM)
        return pl.pallas_call(
            functools.partial(kernel, n),
            out_shape=jax.ShapeDtypeStruct(x.shape, BF16),
            in_specs=[hbm] * 4,
            out_specs=hbm,
            scratch_shapes=[
                pltpu.VMEM(((3 * n - 1) * rc, d_model), BF16),
                pltpu.VMEM((2 * n * rc, ff), BF16),
                pltpu.VMEM((ff, d_model), BF16),
                pltpu.VMEM((SLOTS, d_model, 2 * FT), BF16),
                pltpu.VMEM((rc, d_model), F32),
                pltpu.SemaphoreType.DMA((2, 2 * steps)),
                pltpu.SemaphoreType.DMA((2, 2 * steps)),
                pltpu.SemaphoreType.DMA((2, 2 * steps)),
                pltpu.SemaphoreType.DMA((2, 2 * steps)),
                pltpu.SemaphoreType.DMA((2, SLOTS)),
                pltpu.SemaphoreType.DMA,
                pltpu.SemaphoreType.DMA((2,)),
                pltpu.SemaphoreType.DMA((2,)),
            ],
            compiler_params=pltpu.CompilerParams(
                collective_id=0, has_side_effects=True, vmem_limit_bytes=67043328
            ),
            name="mlp_ring",
        )(x, w_gate, w_up, w_down)

    return jax.shard_map(
        step,
        mesh=mesh,
        in_specs=(P(("dp", "tp"), None), P(None, "tp"), P(None, "tp"), P("tp", None)),
        out_specs=P(("dp", "tp"), None),
        check_vma=False,
    )
```

time: 489 us -> 330 us (0.67)
  waiting for transfers between devices: 345 us -> 0 us
  Pallas kernels: 0 us -> 326 us
  matrix products: 131 us -> 0 us
  between operations: 13.4 us -> 0.01 us
    pallas_call x0 -> x1, Pallas kernels: none -> 326 us  [step(): pl.pallas_call(functools.partial(kernel, n), out_shape=jax.ShapeDtypeStru...]
    all_gather x1 -> x0, waiting for transfers between devices: 175 us -> none  [step(): rows = lax.all_gather(x, 'tp', axis=0, tiled=True)]
    reduce_scatter x1 -> x0, waiting for transfers between devices: 169 us -> none  [step(): return lax.psum_scatter(term, 'tp', scatter_dimension=0, tiled=True)]
    dot_general x3 -> x0, matrix products: 131 us -> none  [the longest x1 46.7 us: step(): up = jnp.dot(rows, w_up, preferred_element_type=jnp.float32)]
  transfers between devices with their start and end apart: 2 -> 0, of which waited for: 2 -> 0; matrix products, arithmetic and copies ran while one was open for 0% -> 0% of each run, Pallas kernels for 0% -> 0%
where the time goes in v2:
time: 330 us
  Pallas kernels  326 us (99%)
    pallas_call x1, Pallas kernels, step(): pl.pallas_call(functools.partial(kernel, n), out_shape=jax.ShapeDtypeStru...  326 us

profile of v2, /device:TPU:21, one launch (start us, length us, event | category | flops | bytes accessed | tf_op | source)
XLA Modules:
  0.0 329.6 jit_solution(13087949440268798164)
XLA Ops:
  0.0 326.5 %mlp_ring.1 = bf16[256,4096]{1,0:T(8,128)(2,1)} custom-call(bf16[256,4096]{1,0:T(8,128)(2,1)} %x_ref.1, bf16[4096,2048]{1,0:T(8,128)(2,1)} %wg_ref.1, bf16[4096,2048]{1,0:T(8,128)(2,1)} %wu_ref.1, bf16[2048,4096]{1,0:T(8,128)(2,1)} %wd_ref.1), custom_call_target="tpu_custom_call" | custom-call | tf_op jit(solution)/shard_map/mlp_ring/pallas_call | solution.py:247
  326.5 3.1 copy.6

commit v3 on v2

--- a/solution.py
+++ b/solution.py
@@ -13,11 +13,12 @@
 FT = 256
 SLOTS = 3
 NT = 512
+VMEM_LIMIT = 51 * 1024 * 1024
 
 
 def kernel(
     n, x_ref, wg_ref, wu_ref, wd_ref, y_ref,
-    buf, hid, wd, wt, own, ag_send, ag_recv, rs_send, rs_recv, w_sem, wd_sem, x_sem, y_sem,
+    buf, hid, wd, wt, own, ag_send, ag_recv, rs_send, rs_recv, w_sem, wd_sem, x_sem,
 ):
     me = lax.axis_index("tp")
     right, left = lax.rem(me + 1, n), lax.rem(me + n - 1, n)
@@ -28,7 +29,8 @@
     ff = wg_ref.shape[1]
     tiles = ff // FT
     per = tiles // 2
-    n_tiles = 2 * n * per
+    halves = 2 * n * per * 2
+    kd = d_model // 2
 
     def rows(block, part=0, size=pc):
         return pl.ds(pl.multiple_of(block * rc + part * pc, pc), size)
@@ -47,7 +49,7 @@
         )
 
     def arrived_sum(c, r):
-        return 2 * n * (1 - c) + r
+        return c * n + r
 
     def rs_copy(d, c, r, block):
         return pltpu.make_async_remote_copy(
@@ -61,9 +63,10 @@
 
     def w_copies(g):
         slot = g % SLOTS
-        col = pl.ds(pl.multiple_of((g % tiles) * FT, FT), FT)
+        row = pl.ds(pl.multiple_of((g % 2) * kd, kd), kd)
+        col = pl.ds(pl.multiple_of((g // 2 % tiles) * FT, FT), FT)
         return [
-            pltpu.make_async_copy(ref.at[:, col], wt.at[slot, :, pl.ds(k * FT, FT)], w_sem.at[k, slot])
+            pltpu.make_async_copy(ref.at[row, col], wt.at[slot, :, pl.ds(k * FT, FT)], w_sem.at[k, slot])
             for k, ref in enumerate((wg_ref, wu_ref))
         ]
 
@@ -101,16 +104,21 @@
         @pl.loop(0, per)
         def _(j):
             g = q * per + j
-            slot = g % SLOTS
-            for copy in w_copies(g):
-                copy.wait()
-
-            @pl.when(g + SLOTS - 1 < n_tiles)
-            def _():
-                for copy in w_copies(g + SLOTS - 1):
-                    copy.start()
-
-            both = jnp.dot(buf[lhs, :], wt[slot], preferred_element_type=F32)
+            both = None
+            for k in range(2):
+                i = 2 * g + k
+                for copy in w_copies(i):
+                    copy.wait()
+
+                @pl.when(i + SLOTS - 1 < halves)
+                def _():
+                    for copy in w_copies(i + SLOTS - 1):
+                        copy.start()
+
+                part = jnp.dot(
+                    buf[lhs, pl.ds(k * kd, kd)], wt[i % SLOTS], preferred_element_type=F32
+                )
+                both = part if both is None else both + part
             gate, up = both[:, :FT], both[:, FT:]
             col = pl.ds(pl.multiple_of((g % tiles) * FT, FT), FT)
             hid[lhs, col] = (jax.nn.silu(gate) * up).astype(BF16)
@@ -144,11 +152,6 @@
     def swapped(block, col):
         return jnp.concatenate([buf[rows(block, 1), col], buf[rows(block, 0), col]], axis=0).astype(F32)
 
-    def y_copy(c):
-        return pltpu.make_async_copy(
-            buf.at[rows(arrived_sum(c, steps - 1), 0, rc)], y_ref.at[pl.ds(c * rc, rc)], y_sem.at[c]
-        )
-
     @pl.loop(0, 4 * steps - 2)
     def _(t):
         @pl.when(t < 2 * steps)
@@ -209,10 +212,9 @@
 
             def body(col):
                 total = down(own_block(0), col) + swapped(last - 1, col) + buf[dst, col].astype(F32)
-                buf[dst, col] = total.astype(BF16)
+                y_ref[pl.ds(0, rc), col] = total.astype(BF16)
 
             down_tiles(body)
-            y_copy(0).start()
 
     wait_sum(1, steps - 2)
     last = arrived_sum(1, steps - 1)
@@ -225,15 +227,12 @@
     wait_sum(1, steps - 1)
 
     def finish(col):
-        buf[dst, col] = (own[:, col] + buf[dst, col].astype(F32)).astype(BF16)
+        y_ref[pl.ds(rc, rc), col] = (own[:, col] + buf[dst, col].astype(F32)).astype(BF16)
 
     down_tiles(finish)
-    y_copy(1).start()
     for u in range(2 * steps - 3, 2 * steps):
         for d in range(2):
             rs_copy(d, u // steps, u % steps, arrived_sum(u // steps, u % steps)).wait_send()
-    for c in range(2):
-        y_copy(c).wait()
 
 
 def solution(mesh):
@@ -248,12 +247,12 @@
             functools.partial(kernel, n),
             out_shape=jax.ShapeDtypeStruct(x.shape, BF16),
             in_specs=[hbm] * 4,
-            out_specs=hbm,
+            out_specs=pl.BlockSpec(memory_space=pltpu.VMEM),
             scratch_shapes=[
-                pltpu.VMEM(((3 * n - 1) * rc, d_model), BF16),
+                pltpu.VMEM((2 * n * rc, d_model), BF16),
                 pltpu.VMEM((2 * n * rc, ff), BF16),
                 pltpu.VMEM((ff, d_model), BF16),
-                pltpu.VMEM((SLOTS, d_model, 2 * FT), BF16),
+                pltpu.VMEM((SLOTS, d_model // 2, 2 * FT), BF16),
                 pltpu.VMEM((rc, d_model), F32),
                 pltpu.SemaphoreType.DMA((2, 2 * steps)),
                 pltpu.SemaphoreType.DMA((2, 2 * steps)),
@@ -262,10 +261,9 @@
                 pltpu.SemaphoreType.DMA((2, SLOTS)),
                 pltpu.SemaphoreType.DMA,
                 pltpu.SemaphoreType.DMA((2,)),
-                pltpu.SemaphoreType.DMA((2,)),
             ],
             compiler_params=pltpu.CompilerParams(
-                collective_id=0, has_side_effects=True, vmem_limit_bytes=67043328
+                collective_id=0, has_side_effects=True, vmem_limit_bytes=VMEM_LIMIT
             ),
             name="mlp_ring",
         )(x, w_gate, w_up, w_down)

time: 330 us -> 327 us (level)
  no operation moved by 1% of the time
where the time goes in v3:
time: 327 us
  Pallas kernels  325 us (99%)
    pallas_call x1, Pallas kernels, step(): pl.pallas_call(functools.partial(kernel, n), out_shape=jax.ShapeDtypeStru...  325 us

profile of v3, /device:TPU:21, one launch (start us, length us, event | category | flops | bytes accessed | tf_op | source)
XLA Modules:
  0.0 326.7 jit_solution(10718581412465477334)
XLA Ops:
  0.0 325.4 %mlp_ring.1 = bf16[256,4096]{1,0:T(8,128)(2,1)S(1)} custom-call(bf16[256,4096]{1,0:T(8,128)(2,1)} %x_ref.1, bf16[4096,2048]{1,0:T(8,128)(2,1)} %wg_ref.1, bf16[4096,2048]{1,0:T(8,128)(2,1)} %wu_ref.1, bf16[2048,4096]{1,0:T(8,128)(2,1)} %wd_ref.1), custom_call_target="tpu_custom_call" | custom-call | tf_op jit(solution)/shard_map/mlp_ring/pallas_call | solution.py:246
  325.4 1.3 copy.6

commit v4 on v2

--- a/solution.py
+++ b/solution.py
@@ -10,14 +10,16 @@
 MESH = pl.DeviceIdType.MESH
 F32 = jnp.float32
 BF16 = jnp.bfloat16
-FT = 256
-SLOTS = 3
-NT = 512
+FT = 128
+SLOTS = 4
+TILT = 8
+NT = 1024
+VMEM_LIMIT = 51 * 1024 * 1024
 
 
 def kernel(
     n, x_ref, wg_ref, wu_ref, wd_ref, y_ref,
-    buf, hid, wd, wt, own, ag_send, ag_recv, rs_send, rs_recv, w_sem, wd_sem, x_sem, y_sem,
+    buf, hid, wd, wt, own, ag_send, ag_recv, rs_send, rs_recv, tilt_sem, w_sem, wd_sem, x_sem,
 ):
     me = lax.axis_index("tp")
     right, left = lax.rem(me + 1, n), lax.rem(me + n - 1, n)
@@ -46,8 +48,33 @@
             device_id_type=MESH,
         )
 
+    far = (1, steps - 1)
+    before_far = 2 * steps - 3
+
+    def short_copy():
+        block = far[0] * n + far[1]
+        return pltpu.make_async_remote_copy(
+            src_ref=buf.at[pl.ds((block - 2) * rc, pc - TILT)],
+            dst_ref=buf.at[pl.ds(block * rc, pc - TILT)],
+            send_sem=ag_send.at[0, 2 * steps - 1],
+            recv_sem=ag_recv.at[0, 2 * steps - 1],
+            device_id={"tp": right},
+            device_id_type=MESH,
+        )
+
+    def tilt_copy():
+        block = far[0] * n + far[1]
+        return pltpu.make_async_remote_copy(
+            src_ref=buf.at[pl.ds(block * rc - TILT, TILT)],
+            dst_ref=buf.at[pl.ds(block * rc + pc - TILT, TILT)],
+            send_sem=tilt_sem.at[0],
+            recv_sem=tilt_sem.at[1],
+            device_id={"tp": left},
+            device_id_type=MESH,
+        )
+
     def arrived_sum(c, r):
-        return 2 * n * (1 - c) + r
+        return c * n + r
 
     def rs_copy(d, c, r, block):
         return pltpu.make_async_remote_copy(
@@ -69,9 +96,10 @@
 
     x_copies = [
         pltpu.make_async_copy(
-            x_ref.at[pl.ds(c * rc, rc)], buf.at[rows(own_block(c), 0, rc)], x_sem.at[c]
+            x_ref.at[pl.ds(c * rc + p * pc, pc)], buf.at[rows(own_block(c), p)], x_sem.at[c, p]
         )
         for c in range(2)
+        for p in range(2)
     ]
     for copy in x_copies:
         copy.start()
@@ -81,14 +109,13 @@
         pl.semaphore_signal(barrier, inc=1, device_id={"tp": neighbour}, device_id_type=MESH)
     pl.semaphore_wait(barrier, 2)
 
-    def send_own(c):
-        for i in range(2):
-            for d in range(2):
-                ag_copy(d, c, i, rows(own_block(c), i ^ d)).start()
-
-    x_copies[0].wait()
-    send_own(0)
-    x_copies[1].wait()
+    for d in range(2):
+        x_copies[d].wait()
+        ag_copy(d, 0, 0, rows(own_block(0), d)).start()
+    for d in range(2):
+        ag_copy(d, 0, 1, rows(own_block(0), 1 - d)).start()
+    for copy in x_copies[2:]:
+        copy.wait()
     for g in range(SLOTS - 1):
         for copy in w_copies(g):
             copy.start()
@@ -101,7 +128,6 @@
         @pl.loop(0, per)
         def _(j):
             g = q * per + j
-            slot = g % SLOTS
             for copy in w_copies(g):
                 copy.wait()
 
@@ -110,7 +136,7 @@
                 for copy in w_copies(g + SLOTS - 1):
                     copy.start()
 
-            both = jnp.dot(buf[lhs, :], wt[slot], preferred_element_type=F32)
+            both = jnp.dot(buf[lhs, :], wt[g % SLOTS], preferred_element_type=F32)
             gate, up = both[:, :FT], both[:, FT:]
             col = pl.ds(pl.multiple_of((g % tiles) * FT, FT), FT)
             hid[lhs, col] = (jax.nn.silu(gate) * up).astype(BF16)
@@ -123,18 +149,27 @@
         def _(j):
             body(pl.ds(pl.multiple_of(j * NT, NT), NT))
 
+    def multiply(block):
+        def body(col):
+            own[:, col] = down(block, col)
+
+        down_tiles(body)
+
     def send_sum(c, r, add):
         block = arrived_sum(c, r - 2) if add else c * n + n - 2 + r
-        dst = rows(block, 0, rc)
-
-        def body(col):
-            term = down(c * n + n - 2 - r, col)
+        for d in range(2):
             if add:
-                term = term + buf[dst, col].astype(F32)
-            buf[dst, col] = term.astype(BF16)
-
-        down_tiles(body)
-        for d in range(2):
+                rs_copy(d, c, r - 2, block).wait_recv()
+            dst = rows(block, d)
+            half = pl.ds(d * pc, pc)
+
+            def body(col):
+                term = own[half, col]
+                if add:
+                    term = term + buf[dst, col].astype(F32)
+                buf[dst, col] = term.astype(BF16)
+
+            down_tiles(body)
             rs_copy(d, c, r, block).start()
 
     def wait_sum(c, r):
@@ -144,33 +179,57 @@
     def swapped(block, col):
         return jnp.concatenate([buf[rows(block, 1), col], buf[rows(block, 0), col]], axis=0).astype(F32)
 
-    def y_copy(c):
-        return pltpu.make_async_copy(
-            buf.at[rows(arrived_sum(c, steps - 1), 0, rc)], y_ref.at[pl.ds(c * rc, rc)], y_sem.at[c]
-        )
-
     @pl.loop(0, 4 * steps - 2)
     def _(t):
         @pl.when(t < 2 * steps)
         def _():
             c, i = t // steps, t % steps
-            for d in range(2):
-                ag_copy(d, c, i, rows(c * n + i, d)).wait_recv()
+            ag_copy(1, c, i, rows(c * n + i, 1)).wait_recv()
 
             @pl.when(i < steps - 2)
             def _():
+                ag_copy(1, c, i + 2, rows(c * n + i, 1)).start()
+
+            @pl.when(t == before_far + 1)
+            def _():
+                tilt_copy().start()
+
+            @pl.when(t < 2 * steps - 1)
+            def _():
+                ag_copy(0, c, i, rows(c * n + i, 0)).wait_recv()
+
+            @pl.when(t == 2 * steps - 1)
+            def _():
+                short_copy().wait_recv()
+
+            @pl.when((i < steps - 2) & (t != before_far))
+            def _():
+                ag_copy(0, c, i + 2, rows(c * n + i, 0)).start()
+
+            @pl.when(t == before_far)
+            def _():
+                short_copy().start()
+
+        @pl.when(t == steps - 2)
+        def _():
+            for i in range(2):
                 for d in range(2):
-                    ag_copy(d, c, i + 2, rows(c * n + i, d)).start()
-
-        @pl.when(t == steps - 2)
-        def _():
-            send_own(1)
+                    ag_copy(d, 1, i, rows(own_block(1), i ^ d)).start()
 
         @pl.when((t >= 1) & (t <= 2 * steps))
         def _():
             a = t - 1
-            for d in range(2):
-                ag_copy(d, a // steps, a % steps, rows((a // steps) * n + a % steps, d)).wait_send()
+            src = (a // steps) * n + a % steps
+            ag_copy(1, a // steps, a % steps, rows(src, 1)).wait_send()
+
+            @pl.when(t < 2 * steps)
+            def _():
+                ag_copy(0, a // steps, a % steps, rows(src, 0)).wait_send()
+
+        @pl.when(t == 2 * steps)
+        def _():
+            short_copy().wait_send()
+            tilt_copy().wait()
 
         @pl.when(t >= 2 * steps + 1)
         def _():
@@ -178,10 +237,6 @@
             for d in range(2):
                 rs_copy(d, u // steps, u % steps, arrived_sum(u // steps, u % steps)).wait_send()
 
-        @pl.when(t == 2 * steps - 2)
-        def _():
-            wd_copy.wait()
-
         @pl.when(t >= 2 * steps - 2)
         def _():
             u = t - (2 * steps - 2)
@@ -193,12 +248,20 @@
 
             @pl.when(r >= 2)
             def _():
-                wait_sum(c, r - 2)
                 send_sum(c, r, True)
 
         @pl.when((t >= 1) & (t <= 2 * n))
         def _():
             hidden_half(t - 1)
+
+        @pl.when(t == 2 * steps - 3)
+        def _():
+            wd_copy.wait()
+
+        @pl.when((t >= 2 * steps - 3) & (t < 4 * steps - 3))
+        def _():
+            u = t - (2 * steps - 3)
+            multiply(u // steps * n + n - 2 - u % steps)
 
         @pl.when(t == 3 * steps - 1)
         def _():
@@ -209,31 +272,30 @@
 
             def body(col):
                 total = down(own_block(0), col) + swapped(last - 1, col) + buf[dst, col].astype(F32)
-                buf[dst, col] = total.astype(BF16)
+                y_ref[pl.ds(0, rc), col] = total.astype(BF16)
 
             down_tiles(body)
-            y_copy(0).start()
-
+
+    multiply(own_block(1))
     wait_sum(1, steps - 2)
     last = arrived_sum(1, steps - 1)
-    dst = rows(last, 0, rc)
 
     def partial(col):
-        own[:, col] = down(own_block(1), col) + swapped(last - 1, col)
+        own[:, col] = own[:, col] + swapped(last - 1, col)
 
     down_tiles(partial)
-    wait_sum(1, steps - 1)
-
-    def finish(col):
-        buf[dst, col] = (own[:, col] + buf[dst, col].astype(F32)).astype(BF16)
-
-    down_tiles(finish)
-    y_copy(1).start()
+    for d in range(2):
+        rs_copy(d, 1, steps - 1, last).wait_recv()
+        half = pl.ds(d * pc, pc)
+
+        def finish(col):
+            y_ref[pl.ds(rc + d * pc, pc), col] = (own[half, col] + buf[rows(last, d), col].astype(F32)).astype(BF16)
+
+        down_tiles(finish)
+
     for u in range(2 * steps - 3, 2 * steps):
         for d in range(2):
             rs_copy(d, u // steps, u % steps, arrived_sum(u // steps, u % steps)).wait_send()
-    for c in range(2):
-        y_copy(c).wait()
 
 
 def solution(mesh):
@@ -248,9 +310,9 @@
             functools.partial(kernel, n),
             out_shape=jax.ShapeDtypeStruct(x.shape, BF16),
             in_specs=[hbm] * 4,
-            out_specs=hbm,
+            out_specs=pl.BlockSpec(memory_space=pltpu.VMEM),
             scratch_shapes=[
-                pltpu.VMEM(((3 * n - 1) * rc, d_model), BF16),
+                pltpu.VMEM((2 * n * rc, d_model), BF16),
                 pltpu.VMEM((2 * n * rc, ff), BF16),
                 pltpu.VMEM((ff, d_model), BF16),
                 pltpu.VMEM((SLOTS, d_model, 2 * FT), BF16),
@@ -259,13 +321,13 @@
                 pltpu.SemaphoreType.DMA((2, 2 * steps)),
                 pltpu.SemaphoreType.DMA((2, 2 * steps)),
                 pltpu.SemaphoreType.DMA((2, 2 * steps)),
+                pltpu.SemaphoreType.DMA((2,)),
                 pltpu.SemaphoreType.DMA((2, SLOTS)),
                 pltpu.SemaphoreType.DMA,
-                pltpu.SemaphoreType.DMA((2,)),
-                pltpu.SemaphoreType.DMA((2,)),
+                pltpu.SemaphoreType.DMA((2, 2)),
             ],
             compiler_params=pltpu.CompilerParams(
-                collective_id=0, has_side_effects=True, vmem_limit_bytes=67043328
+                collective_id=0, has_side_effects=True, vmem_limit_bytes=VMEM_LIMIT
             ),
             name="mlp_ring",
         )(x, w_gate, w_up, w_down)

time: 330 us -> 326 us (0.988)
  no operation moved by 1% of the time
where the time goes in v4:
time: 326 us
  Pallas kernels  324 us (99%)
    pallas_call x1, Pallas kernels, step(): pl.pallas_call(functools.partial(kernel, n), out_shape=jax.ShapeDtypeStru...  324 us

profile of v4, /device:TPU:21, one launch (start us, length us, event | category | flops | bytes accessed | tf_op | source)
XLA Modules:
  0.0 325.7 jit_solution(17144956717355530766)
XLA Ops:
  0.0 324.4 %mlp_ring.1 = bf16[256,4096]{1,0:T(8,128)(2,1)S(1)} custom-call(bf16[256,4096]{1,0:T(8,128)(2,1)} %x_ref.1, bf16[4096,2048]{1,0:T(8,128)(2,1)} %wg_ref.1, bf16[4096,2048]{1,0:T(8,128)(2,1)} %wu_ref.1, bf16[2048,4096]{1,0:T(8,128)(2,1)} %wd_ref.1), custom_call_target="tpu_custom_call" | custom-call | tf_op jit(solution)/shard_map/mlp_ring/pallas_call | solution.py:309
  324.4 1.3 copy.6

commit v5 on v4

--- a/solution.py
+++ b/solution.py
@@ -62,14 +62,18 @@
             device_id_type=MESH,
         )
 
-    def tilt_copy():
+    split = d_model * 3 // 4
+
+    def tilt_copy(d):
         block = far[0] * n + far[1]
+        src = ((block - 2) * rc + pc, block * rc)[d] - TILT
+        col = (pl.ds(split, d_model - split), pl.ds(0, split))[d]
         return pltpu.make_async_remote_copy(
-            src_ref=buf.at[pl.ds(block * rc - TILT, TILT)],
-            dst_ref=buf.at[pl.ds(block * rc + pc - TILT, TILT)],
-            send_sem=tilt_sem.at[0],
-            recv_sem=tilt_sem.at[1],
-            device_id={"tp": left},
+            src_ref=buf.at[pl.ds(src, TILT), col],
+            dst_ref=buf.at[pl.ds(block * rc + pc - TILT, TILT), col],
+            send_sem=tilt_sem.at[0, d],
+            recv_sem=tilt_sem.at[1, d],
+            device_id={"tp": (right, left)[d]},
             device_id_type=MESH,
         )
 
@@ -192,7 +196,7 @@
 
             @pl.when(t == before_far + 1)
             def _():
-                tilt_copy().start()
+                tilt_copy(1).start()
 
             @pl.when(t < 2 * steps - 1)
             def _():
@@ -209,6 +213,7 @@
             @pl.when(t == before_far)
             def _():
                 short_copy().start()
+                tilt_copy(0).start()
 
         @pl.when(t == steps - 2)
         def _():
@@ -229,7 +234,8 @@
         @pl.when(t == 2 * steps)
         def _():
             short_copy().wait_send()
-            tilt_copy().wait()
+            for d in range(2):
+                tilt_copy(d).wait()
 
         @pl.when(t >= 2 * steps + 1)
         def _():
@@ -321,7 +327,7 @@
                 pltpu.SemaphoreType.DMA((2, 2 * steps)),
                 pltpu.SemaphoreType.DMA((2, 2 * steps)),
                 pltpu.SemaphoreType.DMA((2, 2 * steps)),
-                pltpu.SemaphoreType.DMA((2,)),
+                pltpu.SemaphoreType.DMA((2, 2)),
                 pltpu.SemaphoreType.DMA((2, SLOTS)),
                 pltpu.SemaphoreType.DMA,
                 pltpu.SemaphoreType.DMA((2, 2)),

time: 326 us -> 326 us (level)
  no operation moved by 1% of the time
where the time goes in v5:
time: 326 us; the launch traced here: 325 us
  Pallas kernels  324 us (99%)
    pallas_call x1, Pallas kernels, step(): pl.pallas_call(functools.partial(kernel, n), out_shape=jax.ShapeDtypeStru...  324 us

profile of v5, /device:TPU:21, one launch (start us, length us, event | category | flops | bytes accessed | tf_op | source)
XLA Modules:
  0.0 325.4 jit_solution(11870673783621591021)
XLA Ops:
  0.0 324.1 %mlp_ring.1 = bf16[256,4096]{1,0:T(8,128)(2,1)S(1)} custom-call(bf16[256,4096]{1,0:T(8,128)(2,1)} %x_ref.1, bf16[4096,2048]{1,0:T(8,128)(2,1)} %wg_ref.1, bf16[4096,2048]{1,0:T(8,128)(2,1)} %wu_ref.1, bf16[2048,4096]{1,0:T(8,128)(2,1)} %wd_ref.1), custom_call_target="tpu_custom_call" | custom-call | tf_op jit(solution)/shard_map/mlp_ring/pallas_call | solution.py:315
  324.1 1.3 copy.6

commit v6 on v5

--- a/solution.py
+++ b/solution.py
@@ -124,7 +124,7 @@
         for copy in w_copies(g):
             copy.start()
     wd_copy = pltpu.make_async_copy(wd_ref, wd, wd_sem)
-    wd_copy.start()
+    wd_copy.start(priority=1)
 
     def hidden_half(q):
         lhs = pl.ds(pl.multiple_of((q // 2) * 2 * rc, 2 * rc), 2 * rc)
@@ -138,7 +138,7 @@
             @pl.when(g + SLOTS - 1 < n_tiles)
             def _():
                 for copy in w_copies(g + SLOTS - 1):
-                    copy.start()
+                    copy.start(priority=1)
 
             both = jnp.dot(buf[lhs, :], wt[g % SLOTS], preferred_element_type=F32)
             gate, up = both[:, :FT], both[:, FT:]

time: 326 us -> 326 us (level)
  no operation moved by 1% of the time
where the time goes in v6:
time: 326 us; the launch traced here: 325 us
  Pallas kernels  324 us (99%)
    pallas_call x1, Pallas kernels, step(): pl.pallas_call(functools.partial(kernel, n), out_shape=jax.ShapeDtypeStru...  324 us

profile of v6, /device:TPU:21, one launch (start us, length us, event | category | flops | bytes accessed | tf_op | source)
XLA Modules:
  0.0 325.4 jit_solution(7282163438523142115)
XLA Ops:
  0.0 324.1 %mlp_ring.1 = bf16[256,4096]{1,0:T(8,128)(2,1)S(1)} custom-call(bf16[256,4096]{1,0:T(8,128)(2,1)} %x_ref.1, bf16[4096,2048]{1,0:T(8,128)(2,1)} %wg_ref.1, bf16[4096,2048]{1,0:T(8,128)(2,1)} %wu_ref.1, bf16[2048,4096]{1,0:T(8,128)(2,1)} %wd_ref.1), custom_call_target="tpu_custom_call" | custom-call | tf_op jit(solution)/shard_map/mlp_ring/pallas_call | solution.py:315
  324.1 1.3 copy.6
